TPU v7x, 32 devices: a whole 2x2x4 slice. The times are simulated.
32 devices in a mesh: row: 4 (over y, core), grid: 8 (over z, x).
Axes of the slice: x: 2, y: 2, z: 4, core: 2. Of those that a mesh axis runs over, the one named last changes fastest.
Arguments:
- h_rows: bfloat16 [8, 1024, 1024], P('grid', 'row'), may hold values from -6 to 6
- x_blocks: bfloat16 [8, 8, 8, 128, 128], P('grid', 'row'), may hold values from -0.1875 to 0.1875
- x_cols: int32 [8, 8, 8], P('grid', 'row'), may hold values from 0 to 7
- sub_blocks: int32 [4, 8, 3, 6], P('row', 'grid'), may hold values from 0 to 7, as said below
- owners: int32 [4, 8, 3], P('row'), may hold values from 0 to 7, as said below
- shift_mu: float32 [1], replicated, may hold values from -4 to 4
- orbitals: bfloat16 [4, 8, 6, 768, 1536], P('row', 'grid'), may hold values from -0.125 to 0.125
Outputs:
- density: float32 [8, 1024], P('grid', 'row')
Inputs may be any that keep to these rules, and one draw needn't show every extreme that they name: `x_cols`: entries of a block row may repeat; repeated blocks add. `sub_blocks`: the 6 blocks of a submatrix are distinct; the first is its central block. Within each row index, a device's 3 submatrices go to distinct owners, and every owner receives 1 to 6 submatrices.
All inputs are finite; a program needn't handle non-finite values.
Results may differ from a plain program's by a relative error of at most 0.0003.
Values may be sent and summed in bfloat16 or wider, within the bound.
No kernel may reach another device: no remote copies, remote signals or barrier semaphores. Data moves between devices by JAX's collectives and lax.ppermute only.
A program may use at most 128 MiB of HBM per device.

v0:
```python
import jax
import jax.numpy as jnp
from jax import lax
from jax.sharding import PartitionSpec as P

BLK = 128
OWN_MAX = 6
PLANE = 256
DEPTH = 4
MARG = 1
ORDER = 768


def from_behind(value, axis, steps):
    count = lax.axis_size(axis)
    pairs = [(source, (source + steps) % count) for source in range(count)]
    return lax.ppermute(value, axis, pairs)


def densify(blocks, cols, count):
    onehot = (cols[:, :, None] == jnp.arange(count, dtype=jnp.int32)[None, None, :]).astype(
        jnp.bfloat16
    )
    dense = jnp.einsum("rzk,rzab->rakb", onehot, blocks, preferred_element_type=jnp.float32)
    return dense.reshape(blocks.shape[0] * blocks.shape[2], count * blocks.shape[2]).astype(
        jnp.bfloat16
    )


def sign_batch(mats, potential):
    eye = jnp.eye(ORDER, dtype=jnp.float32)
    shifted = mats.astype(jnp.float32) - potential * eye[None]
    scale = jnp.sqrt(jnp.sum(shifted * shifted, axis=(1, 2)) / ORDER + 1e-06)
    first = (shifted / (2.0 * scale)[:, None, None]).astype(jnp.bfloat16)
    square = jnp.einsum("sij,sjk->sik", first, first, preferred_element_type=jnp.float32)
    helper = (3.0 * eye[None] - square).astype(jnp.bfloat16)
    second = (
        0.5 * jnp.einsum("sij,sjk->sik", first, helper, preferred_element_type=jnp.float32)
    ).astype(jnp.bfloat16)
    square_cols = jnp.einsum(
        "sij,sjk->sik", second, second[:, :, :BLK], preferred_element_type=jnp.float32
    )
    helper_cols = (3.0 * eye[None, :, :BLK] - square_cols).astype(jnp.bfloat16)
    last = 0.5 * jnp.einsum("sij,sjk->sik", second, helper_cols, preferred_element_type=jnp.float32)
    return (0.5 * (eye[None, :, :BLK] - last)).astype(jnp.bfloat16)


def on_device(h_rows, x_blocks, x_cols, sub_blocks, owners, shift_mu, orbitals):
    potential = shift_mu[0]
    nreg = h_rows.shape[2]
    count = nreg // BLK
    dense = densify(x_blocks[0], x_cols[0], count)
    product = jnp.dot(
        dense,
        lax.all_gather(h_rows, "row", axis=1, tiled=True)[0],
        preferred_element_type=jnp.float32,
    )
    whole = lax.all_gather(product.astype(jnp.bfloat16), "row", axis=0, tiled=True)
    blocks4 = whole.reshape(count, BLK, count, BLK)

    def extract(picks):
        rows = jnp.take(blocks4, picks, axis=0)
        return jnp.take(rows, picks, axis=2).reshape(ORDER, ORDER)

    mats = jax.vmap(extract)(sub_blocks[0, 0])
    built = sign_batch(mats, potential)
    ngrid = lax.axis_size("grid")
    myself = lax.axis_index("grid")
    table = owners[0]
    targets = lax.dynamic_index_in_dim(table, myself, 0, keepdims=False)
    hit = table == myself
    has = jnp.any(hit, axis=1)
    place = jnp.cumsum(has.astype(jnp.int32)) - 1
    select = has[None, :] & (place[None, :] == jnp.arange(OWN_MAX, dtype=jnp.int32)[:, None])
    selint = select.astype(jnp.int32)
    source = jnp.sum(selint * jnp.arange(ngrid, dtype=jnp.int32)[None, :], axis=1)
    live = jnp.any(select, axis=1)
    outgoing = jnp.zeros((ngrid, ORDER, BLK), jnp.bfloat16).at[targets].set(built)
    incoming = lax.all_to_all(outgoing, "grid", split_axis=0, concat_axis=0, tiled=True)
    columns = jnp.take(incoming, source, axis=0)
    phi = orbitals[0, 0]
    proj = jnp.einsum("tnm,tnx->tmx", columns, phi, preferred_element_type=jnp.float32)
    values = jnp.sum(proj * phi[:, :BLK, :].astype(jnp.float32), axis=1)
    window = jnp.sum(jnp.where(live[:, None], values, 0.0), axis=0).reshape(DEPTH + 2 * MARG, PLANE)
    core = window[MARG : MARG + DEPTH]
    from_prev = from_behind(window[MARG + DEPTH :], "grid", 1)
    from_next = from_behind(window[:MARG], "grid", -1)
    core = core.at[:MARG].add(from_prev)
    core = core.at[DEPTH - MARG :].add(from_next)
    return lax.psum_scatter(core.reshape(1, DEPTH * PLANE), "row", scatter_dimension=1, tiled=True)


def solution(mesh):
    in_specs = (
        P("grid", "row", None),
        P("grid", "row", None, None, None),
        P("grid", "row", None),
        P("row", "grid", None, None),
        P("row", None, None),
        P(),
        P("row", "grid", None, None, None),
    )
    out_specs = P("grid", "row")
    return jax.shard_map(
        on_device, mesh=mesh, in_specs=in_specs, out_specs=out_specs, check_vma=False
    )
```

profile of v0, /device:TPU:0, one launch (start us, length us, event | category | flops | bytes accessed | tf_op | source)
XLA Modules:
  0.0 208.9 jit_solution(14738426519535640301)
XLA Ops:
  6.5 0.7 all-gather.3.cloned.1.call-update
  7.3 0.3 copy-done
  7.6 1.1 convolution_convert_fusion
  8.7 25.6 %all-gather.3.cloned.1.call-done = bf16[1,1024,1024]{2,1,0:T(8,128)(2,1)} async-done(((bf16[1,256,1024]{2,1,0:T(8,128)(2,1)}), bf16[1,1024,1024]{2,1,0:T(8,128)(2,1)}) %all-gather.3.cloned.1.call-update) | async-done | bytes 2097168 | tf_op jit(solution)/shard_map/all_gather | solution.py:55
  34.2 3.1 %fusion.10 = bf16[256,1024]{1,0:T(8,128)(2,1)} fusion(bf16[1,1024,1024]{2,1,0:T(8,128)(2,1)} %all-gather.3.cloned.1.call-done, bf16[32,8,8,128]{3,2,1,0:T(8,128)(2,1)S(1)} %bitcast.77), kind=kOutput, calls=%fused_computation.23 | convolution fusion | flops 537133056 | bytes 3145728 | tf_op jit(solution)/shard_map/dot_general | solution.py:53
  38.8 2.5 %fusion.13 = (f32[768,768]{1,0:T(8,128)}, f32[768,768]{1,0:T(8,128)}) fusion(f32[]{:T(128)} %bitcast.69), kind=kLoop, calls=%fused_computation.25 | loop fusion | flops 1769472 | bytes 4718596 | tf_op jit(solution)/shard_map/mul | solution.py:36
  41.3 0.8 slice_select_fusion
  42.1 1.7 compare_select_fusion
  43.8 16.3 %all-gather.5.cloned.1.call-done = bf16[1024,1024]{1,0:T(8,128)(2,1)} async-done(((bf16[256,1024]{1,0:T(8,128)(2,1)}), bf16[1024,1024]{1,0:T(8,128)(2,1)}) %all-gather.5.cloned.1.call-update) | async-done | bytes 2097168 | tf_op jit(solution)/shard_map/all_gather | solution.py:58
  60.1 2.2 %copy.28 = bf16[128,8,8,128]{3,2,1,0:T(8,128)(2,1)S(1)} copy(bf16[128,8,8,128]{3,1,2,0:T(8,128)(2,1)} %bitcast.76) | data formatting | bytes 4194304
  62.3 3.9 %gather_fusion = bf16[18,128,8,128]{3,2,1,0:T(8,128)(2,1)} fusion(bf16[8,128,8,128]{3,2,1,0:T(8,128)(2,1)S(1)} %bitcast.74, s32[1024]{0:T(1024)S(1)} %pad_clamp_fusion.1), kind=kCustom, calls=%fused_computation | custom fusion | bytes 9437256 | tf_op jit(solution)/shard_map/vmap(jit(_take))/gather | solution.py:62
  66.2 3.7 %copy.18 = bf16[18,128,8,128]{3,1,2,0:T(8,128)(2,1)S(1)} copy(bf16[18,128,8,128]{3,2,1,0:T(8,128)(2,1)} %gather_fusion) | data formatting | bytes 9437184 | tf_op jit(solution)/shard_map/vmap(jit(_take))/gather | solution.py:62
  69.9 2.6 %broadcast_select_fusion = bf16[3,6,128,8,128]{4,2,3,1,0:T(8,128)(2,1)} fusion(bf16[3,6,128,8,128]{4,2,3,1,0:T(8,128)(2,1)S(1)} %bitcast.75, pred[3,6]{1,0:T(4,128)(4,1)S(1)} %compare_and_fusion), kind=kLoop, calls=%fused_computation.9 | loop fusion | flops 2359296 | bytes 9437202 | tf_op jit(solution)/shard_map/vmap(jit(_take))/select_n | solution.py:62
  72.6 5.5 %gather_fusion.2 = bf16[18,6,128,128]{3,2,1,0:T(8,128)(2,1)} fusion(bf16[3,6,128,8,128]{4,2,3,1,0:T(8,128)(2,1)} %broadcast_select_fusion, s32[18]{0:T(128)S(1)} %reshape.244), kind=kCustom, calls=%fused_computation.2 | custom fusion | bytes 7078032 | tf_op jit(solution)/shard_map/vmap(jit(_take))/gather | solution.py:63
  78.0 7.3 %copy.19 = bf16[3,6,128,6,128]{4,3,2,1,0:T(8,128)(2,1)} copy(bf16[3,6,128,6,128]{4,2,1,3,0:T(8,128)(2,1)} %bitcast.72) | data formatting | bytes 7077888 | tf_op jit(solution)/shard_map/vmap(jit(_take))/gather | solution.py:63
  85.3 1.6 multiply_reduce_fusion
  87.0 8.4 %gather.16 = bf16[3,768,768]{2,1,0:T(8,128)(2,1)} reshape(bf16[3,6,128,6,128]{4,3,2,1,0:T(8,128)(2,1)} %copy.19) | data formatting | bytes 7077888 | tf_op jit(solution)/shard_map/vmap(jit(_take))/gather | solution.py:63
  95.4 14.7 %multiply_convert_fusion = bf16[3,768,768]{2,1,0:T(8,128)(2,1)} fusion(f32[768,768]{1,0:T(8,128)S(1)} %copy-done.3, f32[3]{0:T(128)S(1)} %sqrt_multiply_fusion, f32[768,768]{1,0:T(8,128)} %get-tuple-element.35, bf16[3,768,768]{2,1,0:T(8,128)(2,1)} %gather.16, pred[3,768]{1,0:T(4,128)(4,1)S(1)} %bitcast.82), kind=kOutput, calls=%fused_computation.4 | convolution fusion | flops 5460590592 | bytes 11798796 | tf_op jit(solution)/shard_map/sij,sjk->sik/dot_general | solution.py:38
  110.1 5.2 %fusion.9 = bf16[3,768,128]{2,1,0:T(8,128)(2,1)S(1)} fusion(bf16[3,768,768]{2,1,0:T(8,128)(2,1)} %multiply_convert_fusion, f32[768,128]{1,0:T(8,128)} %slice_select_fusion, f32[768,128]{1,0:T(8,128)S(1)} %slice_convert_fusion), kind=kOutput, calls=%fused_computation.22 | convolution fusion | flops 907739136 | bytes 9043968 | tf_op jit(solution)/shard_map/sij,sjk->sik/dot_general | solution.py:44
  115.3 1.4 broadcast_in_dim.67
  116.7 2.6 %scatter_fusion = bf16[8,768,128]{2,1,0:T(8,128)(2,1)} fusion(bf16[8,768,128]{2,1,0:T(8,128)(2,1)} %broadcast_in_dim.67, s32[3]{0:T(128)S(1)} %fusion.29, bf16[3,768,128]{2,1,0:T(8,128)(2,1)S(1)} %fusion.9), kind=kCustom, calls=%fused_computation.3 | custom fusion | bytes 1769484 | tf_op jit(solution)/shard_map/scatter | solution.py:78
  119.3 5.5 %all-to-all-start = ((bf16[8,768,128]{2,1,0:T(8,128)(2,1)}), bf16[8,768,128]{2,1,0:T(8,128)(2,1)S(1)}, u32[]{:S(2)}, u32[]{:S(2)}) async-start(bf16[8,768,128]{2,1,0:T(8,128)(2,1)} %scatter_fusion), calls=%async_computation | async-start | bytes 3145728 | tf_op jit(solution)/shard_map/all_to_all | solution.py:79
  125.4 36.8 %all-to-all-done = bf16[8,768,128]{2,1,0:T(8,128)(2,1)S(1)} async-done(((bf16[8,768,128]{2,1,0:T(8,128)(2,1)}), bf16[8,768,128]{2,1,0:T(8,128)(2,1)S(1)}, u32[]{:S(2)}, u32[]{:S(2)}) %all-to-all-start) | async-done | bytes 1572896 | tf_op jit(solution)/shard_map/all_to_all | solution.py:79
  162.2 0.8 gather_fusion.1
  163.0 7.9 %multiply_reduce_fusion.1 = f32[6,1536]{1,0:T(8,128)S(1)} fusion(bf16[6,768,1536]{2,1,0:T(8,128)(2,1)} %bitcast.86, bf16[6,768,128]{2,1,0:T(8,128)(2,1)S(1)} %gather_fusion.1, pred[6]{0:T(512)(128)(4,1)S(1)} %compare_and_fusion.1), kind=kOutput, calls=%fused_computation.8 | convolution fusion | flops 1816058880 | bytes 17731590 | tf_op jit(solution)/shard_map/tnm,tnx->tmx/dot_general | solution.py:82
  171.0 1.5 collective-permute-start
  172.5 3.3 %collective-permute-start.1 = (f32[1,256]{1,0:T(1,128)S(1)}, f32[1,256]{1,0:T(1,128)S(1)}, u32[]{:S(2)}, u32[]{:S(2)}) collective-permute-start(f32[1,256]{1,0:T(1,128)S(1)} %bitcast.84), channel_id=1, source_target_pairs={{0,7},{1,0},{2,1},{3,2},{4,3},{5,4},{6,5},{7,6},{8,15},{9,8},{10,9... | collective-permute-start | bytes 3080 | tf_op jit(solution)/shard_map/ppermute | solution.py:17
  175.8 1.5 collective-permute-done
  177.4 0.2 copy.30
  177.7 0.8 bitcast_bitcast_fusion
  178.5 22.3 %reduce-scatter.4.cloned.1.call-done = f32[256,1]{1,0:T(8,128)} async-done(((f32[1024,1]{1,0:T(8,128)}), f32[256,1]{1,0:T(8,128)}) %reduce-scatter.4.cloned.1.call-update) | async-done | bytes 1040
  200.8 1.5 copy.24
  (48 shorter events, 1.6 us)
Async XLA Ops:
  6.5 1.0 copy-start
  6.5 30.8 %copy-start.5 = (s32[1,1,3,6]{3,1,2,0:T(1,128)S(1)}, s32[1,1,3,6]{3,1,2,0:T(1,128)}, u32[]{:S(2)}) copy-start(s32[1,1,3,6]{3,1,2,0:T(1,128)} %param.14) | copy-start | bytes 220
  6.5 31.8 %copy-start.4 = (s32[1,8,3]{1,0,2:T(1,128)S(1)}, s32[1,8,3]{1,0,2:T(1,128)}, u32[]{:S(2)}) copy-start(s32[1,8,3]{1,0,2:T(1,128)} %param.15) | copy-start | bytes 292
  6.5 27.7 %all-gather.3.cloned.1.call-start = ((), (), s32[]{:S(2)}) async-start(), calls=%async_computation.2 | async-start | bytes 2621440 | tf_op jit(solution)/shard_map/all_gather | solution.py:55
  7.3 52.8 %all-gather.5.cloned.1.call-start = ((), (), s32[]{:S(2)}) async-start(), calls=%async_computation.3 | async-start | bytes 2621440 | tf_op jit(solution)/shard_map/all_gather | solution.py:58
  78.0 7.3 %copy-start.1 = (bf16[18,6,128,128]{3,2,1,0:T(8,128)(2,1)S(1)}, bf16[18,6,128,128]{3,2,1,0:T(8,128)(2,1)}, u32[]{:S(2)}) copy-start(bf16[18,6,128,128]{3,2,1,0:T(8,128)(2,1)} %gather_fusion.2) | copy-start | bytes 10616836
  78.0 7.3 %copy-start.2 = (f32[6,128,6,128]{3,1,0,2:T(8,128)S(1)}, f32[6,128,6,128]{3,1,0,2:T(8,128)}, u32[]{:S(2)}) copy-start(f32[6,128,6,128]{3,1,0,2:T(8,128)} %compare_select_fusion) | copy-start | bytes 7077892
  87.0 8.4 %copy-start.3 = (f32[768,768]{1,0:T(8,128)S(1)}, f32[768,768]{1,0:T(8,128)}, u32[]{:S(2)}) copy-start(f32[768,768]{1,0:T(8,128)} %get-tuple-element.34) | copy-start | bytes 7077892
  119.3 42.9 %all-to-all-start = ((bf16[8,768,128]{2,1,0:T(8,128)(2,1)}), bf16[8,768,128]{2,1,0:T(8,128)(2,1)S(1)}, u32[]{:S(2)}, u32[]{:S(2)}) async-start(bf16[8,768,128]{2,1,0:T(8,128)(2,1)} %scatter_fusion), calls=%async_computation | async-start | bytes 3145728 | tf_op jit(solution)/shard_map/all_to_all | solution.py:79
  124.9 75.9 %reduce-scatter.4.cloned.1.call-start = ((), (), s32[]{:S(2)}) async-start(), calls=%async_computation.4 | async-start | bytes 655360
  171.0 6.3 %collective-permute-start = (f32[1,256]{1,0:T(1,128)S(1)}, f32[1,256]{1,0:T(1,128)S(1)}, u32[]{:S(2)}, u32[]{:S(2)}) collective-permute-start(f32[1,256]{1,0:T(1,128)S(1)} %bitcast.85), channel_id=1, source_target_pairs={{0,1},{1,2},{2,3},{3,4},{4,5},{5,6},{6,7},{7,0},{8,9},{9,10},{10,1... | collective-permute-start | bytes 3080 | tf_op jit(solution)/shard_map/ppermute | solution.py:17
  172.5 4.8 %collective-permute-start.1 = (f32[1,256]{1,0:T(1,128)S(1)}, f32[1,256]{1,0:T(1,128)S(1)}, u32[]{:S(2)}, u32[]{:S(2)}) collective-permute-start(f32[1,256]{1,0:T(1,128)S(1)} %bitcast.84), channel_id=1, source_target_pairs={{0,7},{1,0},{2,1},{3,2},{4,3},{5,4},{6,5},{7,6},{8,15},{9,8},{10,9... | collective-permute-start | bytes 3080 | tf_op jit(solution)/shard_map/ppermute | solution.py:17
Sparse Core Ops, SparseCore 0:
  8.9 25.2 all-gather.2
  37.5 22.5 all-gather.4
  178.6 22.0 reduce-scatter.3
where the time goes:
time: 209 us
  waiting for transfers between devices  103 us (49%)
  local copies, waits for them, and re-layouts  39.2 us (19%)
  matrix products  32 us (15%)
  between operations  13.9 us (7%)
  starting transfers between devices  10.4 us (5%)
  other arithmetic  10.2 us (5%)
    all_to_all x1, waiting for transfers between devices, on_device(): lax.all_to_all(outgoing, 'grid', split_axis=0, concat_axis=0, tiled=True)  36.8 us
    all_gather x1, waiting for transfers between devices, on_device(): lax.all_gather(h_rows, 'row', axis=1, tiled=True)[0]  25.6 us
    unnamed x4, waiting for transfers between devices  23 us
    gather x4, local copies, waits for them, and re-layouts, extract(): return jnp.take(rows, picks, axis=2).reshape(ORDER, ORDER)  21.3 us
    all_gather x1, waiting for transfers between devices, on_device(): lax.all_gather(product.astype(jnp.bfloat16), 'row', axis=0, tiled=True)  16.3 us
    dot_general x1, matrix products, sign_batch(): jnp.einsum('sij,sjk->sik', first, helper, preferred_element_type=jnp.floa...  14.7 us
    dot_general x1, matrix products, on_device(): jnp.einsum('tnm,tnx->tmx', columns, phi, preferred_element_type=jnp.float32)  7.92 us
    gather x2, local copies, waits for them, and re-layouts, extract(): rows = jnp.take(blocks4, picks, axis=0)  7.62 us
  transfers between devices with their start and end apart: 6, of which 5 were waited for; matrix products, arithmetic and copies ran while one was open for 4% of the time, Pallas kernels for 0%

commit v1 on v0

v1 whole, which is shorter than its diff:
```python
import jax
import jax.numpy as jnp
from jax import lax
from jax.experimental import pallas as pl
from jax.experimental.pallas import tpu as pltpu
from jax.sharding import PartitionSpec as P


BLK = 128
PLANE = 256
DEPTH = 4
MARG = 1
ORDER = 768
SUB_BLK = ORDER // BLK


def densify(blocks, cols, count):
    onehot = (cols[:, :, None] == jnp.arange(count, dtype=jnp.int32)[None, None, :]).astype(
        jnp.bfloat16
    )
    dense = jnp.einsum("rzk,rzab->rakb", onehot, blocks, preferred_element_type=jnp.float32)
    return dense.reshape(blocks.shape[0] * blocks.shape[2], count * blocks.shape[2]).astype(
        jnp.bfloat16
    )


def across_chips(value, steps):
    count = lax.axis_size("row")
    pairs = [(src, (src + 2 * steps) % count) for src in range(count)]
    return lax.ppermute(value, "row", pairs)


def across_cores(value):
    return flipped(value, "row", 1)


def flipped(value, axis, mask):
    count = lax.axis_size(axis)
    return lax.ppermute(value, axis, [(src, src ^ mask) for src in range(count)])


def eye_tile(rows, cols):
    r = lax.broadcasted_iota(jnp.int32, (rows, cols), 0)
    c = lax.broadcasted_iota(jnp.int32, (rows, cols), 1)
    return r == c


def wide_dot(a, b):
    return jnp.dot(a, b, preferred_element_type=jnp.float32)


def product_rows(x, srcs, hs, prod, squares, row0, ready=None):
    rows = x.shape[0]
    acc = None
    for j in reversed(range(len(hs))):
        if j == 0 and ready is not None:
            ready()
        at = pl.multiple_of(srcs[j] * rows, rows)
        part = wide_dot(x[:, pl.ds(at, rows)], hs[j][...])
        acc = part if acc is None else acc + part
    acc = acc.astype(jnp.bfloat16)
    prod[row0 : row0 + rows, :] = acc
    for a in range(rows // BLK):
        for b in range(acc.shape[1] // BLK):
            block = acc[a * BLK : (a + 1) * BLK, b * BLK : (b + 1) * BLK].astype(jnp.float32)
            squares[row0 // BLK + a, b] = jnp.sum((block * block).reshape(-1, 8, BLK), axis=0)


def early_kernel(nrow, srcs, *refs):
    hs = refs[:nrow]
    xs = refs[nrow:-2]
    prod, squares = refs[-2:]
    for i, x in enumerate(xs):
        product_rows(x, srcs, hs, prod, squares, i * x.shape[0])


def sign_kernel(nrow, ngrid, nsub, meta, mu, *refs):
    at_picks = nrow
    at_rows = at_picks + nsub * SUB_BLK
    at_shift = at_rows + nsub * SUB_BLK
    srcs = meta
    h_own, *hs = refs[:nrow]
    xa, xb, prod_early, squares_early = refs[nrow : nrow + 4]
    outs = refs[nrow + 4 : nrow + 4 + ngrid]
    prod, squares, shifted, square, column, h_near, sems = refs[nrow + 4 + ngrid :]
    hs = [h_near] + hs
    rows = xa.shape[0]
    early = prod_early.shape[0]
    loads = [
        pltpu.make_async_copy(h_own, h_near, sems.at[0]),
        pltpu.make_async_copy(prod_early, prod.at[pl.ds(0, early)], sems.at[1]),
        pltpu.make_async_copy(squares_early, squares.at[pl.ds(0, early // BLK)], sems.at[2]),
    ]
    for load in loads:
        load.start()

    def ready():
        for load in loads:
            load.wait()

    product_rows(xa, srcs, hs, prod, squares, early, ready)
    product_rows(xb, srcs, hs, prod, squares, early + rows)
    potential = mu[0]
    halves = []
    for k in range(nsub):
        total = jnp.zeros((8, BLK), jnp.float32)
        for a in range(SUB_BLK):
            ra = meta[at_rows + k * SUB_BLK + a]
            for b in range(SUB_BLK):
                cb = meta[at_picks + k * SUB_BLK + b]
                block = prod[
                    pl.ds(pl.multiple_of(ra * BLK, BLK), BLK),
                    pl.ds(pl.multiple_of(cb * BLK, BLK), BLK),
                ]
                if a == b:
                    wide = block.astype(jnp.float32)
                    wide = jnp.where(eye_tile(BLK, BLK), wide - potential, wide)
                    block = wide.astype(jnp.bfloat16)
                    total = total + jnp.sum((wide * wide).reshape(-1, 8, BLK), axis=0)
                else:
                    total = total + squares[ra, cb]
                shifted[k, a * BLK : (a + 1) * BLK, b * BLK : (b + 1) * BLK] = block
        norm = jnp.sum(jnp.sum(total, axis=0, keepdims=True), axis=1, keepdims=True)
        half = 0.5 * lax.rsqrt(norm / ORDER + 1e-06)
        halves.append(half)
        square[k] = ((half * half) * wide_dot(shifted[k], shifted[k])).astype(jnp.bfloat16)
    firsts = []
    for k in range(nsub):
        start = shifted[k, :, :BLK]
        firsts.append(3.0 * start.astype(jnp.float32) - wide_dot(square[k], start))
    seconds = firsts
    for _ in range(2):
        seconds = [
            3.0 * seconds[k] - wide_dot(square[k], seconds[k].astype(jnp.bfloat16))
            for k in range(nsub)
        ]
    unit = jnp.where(eye_tile(ORDER, BLK), 0.5, 0.0)
    for k in range(nsub):
        last = wide_dot(square[k], seconds[k].astype(jnp.bfloat16))
        sign = (0.125 * halves[k]) * (3.0 * firsts[k] - 0.25 * last)
        column[k] = (unit - sign).astype(jnp.bfloat16)
        for s in range(ngrid):

            @pl.when(meta[at_shift + k] == s)
            def _(k=k, s=s):
                outs[s][...] = column[k]


SMEM = pl.BlockSpec(memory_space=pltpu.SMEM)
VMEM = pl.BlockSpec(memory_space=pltpu.VMEM)
HBM = pl.BlockSpec(memory_space=pltpu.HBM)


def grant(count):
    return pltpu.CompilerParams(vmem_limit_bytes=count)


def work(flops):
    return pl.CostEstimate(flops=flops, transcendentals=0, bytes_accessed=flops // 256)


def early_product(srcs, hs, xs):
    rows, nreg = xs[0].shape
    total = rows * len(xs)
    return pl.pallas_call(
        lambda *refs: early_kernel(len(hs), *refs),
        out_shape=(
            jax.ShapeDtypeStruct((total, nreg), jnp.bfloat16),
            jax.ShapeDtypeStruct((total // BLK, nreg // BLK, 8, BLK), jnp.float32),
        ),
        in_specs=[SMEM] + [VMEM] * (len(hs) + len(xs)),
        out_specs=(VMEM, VMEM),
        compiler_params=grant((8 << 20) + 6 * nreg * nreg),
        cost_estimate=work(2 * total * nreg * nreg),
        name="early",
    )(srcs, *hs, *xs)


def sign_columns(meta, mu, hs, xs, prod, squares, ngrid, nsub):
    rows, nreg = xs[0].shape
    return pl.pallas_call(
        lambda *refs: sign_kernel(len(hs), ngrid, nsub, *refs),
        out_shape=[jax.ShapeDtypeStruct((ORDER, BLK), jnp.bfloat16)] * ngrid,
        in_specs=[SMEM] * 2 + [HBM] + [VMEM] * (len(hs) - 1 + len(xs)) + [HBM] * 2,
        out_specs=[VMEM] * ngrid,
        scratch_shapes=[
            pltpu.VMEM((nreg, nreg), jnp.bfloat16),
            pltpu.VMEM((nreg // BLK, nreg // BLK, 8, BLK), jnp.float32),
            pltpu.VMEM((nsub, ORDER, ORDER), jnp.bfloat16),
            pltpu.VMEM((nsub, ORDER, ORDER), jnp.bfloat16),
            pltpu.VMEM((nsub, ORDER, BLK), jnp.bfloat16),
            pltpu.VMEM((rows, nreg), jnp.bfloat16),
            pltpu.SemaphoreType.DMA((3,)),
        ],
        compiler_params=grant((28 << 20) + 6 * nreg * nreg),
        cost_estimate=work(6 * nsub * ORDER**3),
        name="sign",
    )(meta, mu, *hs, *xs, prod, squares)


def collocate(cols, phi, acc):
    proj = lax.dot_general(
        cols, phi, (((0,), (0,)), ((), ())), preferred_element_type=jnp.float32
    )
    values = proj * phi[:BLK, :].astype(jnp.float32)
    acc[...] += jnp.sum(values, axis=0, keepdims=True)


def first_kernel(at, total, meta, orbitals, *refs):
    count = refs[-2].shape[0]
    cols = refs[:count]
    acc, rest, phi, sems = refs[count:]
    live = [meta[at + i] for i in range(total)]
    slots = [meta[at + total + i] for i in range(total)]

    def fetch(i):
        target = phi.at[i] if i < count else rest.at[i - count]
        return pltpu.make_async_copy(orbitals.at[slots[i]], target, sems.at[i])

    for i in range(total):

        @pl.when(live[i] > 0)
        def _(i=i):
            fetch(i).start()

    acc[...] = jnp.zeros_like(acc)
    for i in range(total):

        @pl.when(live[i] > 0)
        def _(i=i):
            fetch(i).wait()
            if i < count:
                collocate(cols[i][...], phi[i], acc)


def next_kernel(at, first, base, meta, before, phi, *refs):
    *cols, acc = refs
    acc[...] = before[...]
    for i in range(len(cols)):

        @pl.when(meta[at + first + i] > 0)
        def _(i=i):
            collocate(cols[i][...], phi[first - base + i], acc)


def last_kernel(at, first, base, count, nrow, edge, meta, before, phi, *refs):
    cols = refs[:count]
    acc = refs[-1]
    outs = refs[count:-1]
    next_kernel(at, first, base, meta, before, phi, *cols, acc)
    me = meta[0]
    chunk = outs[0].shape[1]
    for s in range(nrow // 2):
        for c in range(2):
            peer = me ^ (2 * s + c)
            core = edge + peer
            end = jnp.where(peer < edge, edge + nrow + peer, jnp.maximum(peer - (nrow - edge), 0))
            for i, start in enumerate((core, end)):
                piece = acc[:, pl.ds(pl.multiple_of(start * chunk, chunk), chunk)]
                outs[s][2 * c + i : 2 * c + i + 1, :] = piece


def first_windows(at, total, cols, meta, orbitals):
    shape = orbitals.shape[1:]
    count = len(cols)
    size = shape[0] * shape[1] * 2
    return pl.pallas_call(
        lambda *refs: first_kernel(at, total, *refs),
        out_shape=(
            jax.ShapeDtypeStruct((1, shape[1]), jnp.float32),
            jax.ShapeDtypeStruct((total - count,) + shape, jnp.bfloat16),
        ),
        in_specs=[SMEM, HBM] + [VMEM] * count,
        out_specs=(VMEM, VMEM),
        scratch_shapes=[
            pltpu.VMEM((count,) + shape, jnp.bfloat16),
            pltpu.SemaphoreType.DMA((total,)),
        ],
        compiler_params=grant((6 << 20) + total * size),
        cost_estimate=work(2 * count * BLK * size),
        name="first",
    )(meta, orbitals, *cols)


def next_windows(at, first, base, cols, meta, before, phi):
    return pl.pallas_call(
        lambda *refs: next_kernel(at, first, base, *refs),
        out_shape=jax.ShapeDtypeStruct(before.shape, jnp.float32),
        in_specs=[SMEM] + [VMEM] * (2 + len(cols)),
        out_specs=VMEM,
        compiler_params=grant(18 << 20),
        name="next",
    )(meta, before, phi, *cols)


def last_windows(at, first, base, cols, meta, before, phi, nrow, edge):
    chunk = DEPTH * PLANE // nrow
    return pl.pallas_call(
        lambda *refs: last_kernel(at, first, base, len(cols), nrow, edge, *refs),
        out_shape=[jax.ShapeDtypeStruct((4, chunk), jnp.float32)] * (nrow // 2),
        in_specs=[SMEM] + [VMEM] * (2 + len(cols)),
        out_specs=[VMEM] * (nrow // 2),
        scratch_shapes=[pltpu.VMEM(before.shape, jnp.float32)],
        compiler_params=grant(18 << 20),
        name="last",
    )(meta, before, phi, *cols)


def send_order(ngrid):
    half = ngrid // 2
    near = list(range(2, half)) + [1]
    far = list(range(half, ngrid))
    return far[:1] + near + far[1:]


def on_device(h_rows, x_blocks, x_cols, sub_blocks, owners, shift_mu, orbitals):
    nrow = lax.axis_size("row")
    ngrid = lax.axis_size("grid")
    nchip = nrow // 2
    rows, nreg = h_rows.shape[1:]
    count = nreg // BLK
    me = lax.axis_index("row")
    myself = lax.axis_index("grid")

    h_own = h_rows[0]
    x_own = densify(x_blocks[0], x_cols[0], count)
    hs = []
    for s in range(nchip):
        h = across_chips(h_own, s) if s else h_own
        hs += [h, across_cores(h)]
    xs = []
    for s in range(nchip):
        x = across_chips(x_own, s) if s else x_own
        xs += [x, across_cores(x)]
    order = jnp.arange(nrow, dtype=jnp.int32)
    srcs = (me // 2 * 2 - order // 2 * 2) % nrow + (me + order) % 2

    picks = sub_blocks[0, 0]
    per = rows // BLK
    chip = picks // per
    rowpicks = ((me // 2 - chip // 2) % nchip * 2 + (chip + me) % 2) * per + picks % per

    table = owners[0]
    targets = lax.dynamic_index_in_dim(table, myself, 0, keepdims=False)
    steps = jnp.arange(ngrid, dtype=jnp.int32)
    has = jnp.any(table == myself, axis=1)
    place = jnp.sum(((steps[None, :] < steps[:, None]) & has[None, :]).astype(jnp.int32), axis=1)
    pair = (steps[None, :] == (steps ^ myself)[:, None]) & has[None, :]
    live = jnp.sum(pair.astype(jnp.int32), axis=1)
    slots = jnp.sum(pair.astype(jnp.int32) * place[None, :], axis=1)
    meta = jnp.concatenate(
        [srcs, picks.reshape(-1), rowpicks.reshape(-1), targets ^ myself, live, slots]
    )
    nsub = picks.shape[0]
    at = nrow + 2 * nsub * SUB_BLK + nsub

    prod, squares = early_product(meta, hs, xs[:-2])
    outgoing = sign_columns(meta, shift_mu, hs, xs[-2:], prod, squares, ngrid, nsub)

    arrived = {0: outgoing[0]}
    for s in send_order(ngrid):
        arrived[s] = flipped(outgoing[s], "grid", s)

    edge = MARG * nrow // DEPTH
    cuts = (ngrid - 3, ngrid - 1)
    got = [arrived[s] for s in range(ngrid)]
    partial, phi = first_windows(at, ngrid, got[: cuts[0]], meta, orbitals[0, 0])
    partial = next_windows(
        at, cuts[0], cuts[0], got[cuts[0] : cuts[1]], meta, partial, phi
    )
    parts = last_windows(at, cuts[1], cuts[0], got[cuts[1] :], meta, partial, phi, nrow, edge)
    total = parts[0]
    for s in range(1, nchip):
        total = total + flipped(parts[s], "row", 2 * s)
    both = total[:2] + across_cores(total[2:])
    pairs = [
        (p * ngrid + o, p * ngrid + (o + step) % ngrid)
        for first, step in ((0, 1), (nrow - edge, -1))
        for p in range(first, first + edge)
        for o in range(ngrid)
    ]
    return both[:1] + lax.ppermute(both[1:], ("row", "grid"), pairs)


def solution(mesh):
    in_specs = (
        P("grid", "row", None),
        P("grid", "row", None, None, None),
        P("grid", "row", None),
        P("row", "grid", None, None),
        P("row", None, None),
        P(),
        P("row", "grid", None, None, None),
    )
    out_specs = P("grid", "row")
    return jax.shard_map(
        on_device, mesh=mesh, in_specs=in_specs, out_specs=out_specs, check_vma=False
    )
```

time: 209 us -> 96.2 us (0.46)
  the two profiles are of different devices: /device:TPU:0 before, /device:TPU:16 now
where the time goes in v1:
time: 96.2 us; the launch traced here: 95.8 us
  waiting for transfers between devices  56 us (58%)
  Pallas kernels  17.7 us (18%)
  starting transfers between devices  14.7 us (15%)
  other arithmetic  3.24 us (3%)
  local copies, waits for them, and re-layouts  2.37 us (2%)
  matrix products  1.08 us (1%)
    ppermute x13, waiting for transfers between devices, flipped(): lax.ppermute(value, axis, [(src, src ^ mask) for src in range(count)])  33.9 us
    ppermute x2, waiting for transfers between devices, across_chips(): return lax.ppermute(value, 'row', pairs)  17.6 us
    pallas_call x1, Pallas kernels, sign_columns(): pl.pallas_call(lambda *refs: sign_kernel(len(hs), ngrid, nsub, *refs), ou...  11.4 us
    ppermute x13, starting transfers between devices, flipped(): lax.ppermute(value, axis, [(src, src ^ mask) for src in range(count)])  10.1 us
    ppermute x1, waiting for transfers between devices, on_device(): return both[:1] + lax.ppermute(both[1:], ('row', 'grid'), pairs)  4.42 us
    ppermute x2, starting transfers between devices, across_chips(): return lax.ppermute(value, 'row', pairs)  2.62 us
    pallas_call x1, Pallas kernels, early_product(): pl.pallas_call(lambda *refs: early_kernel(len(hs), *refs), out_shape=(jax...  2.49 us
    unnamed x15, local copies, waits for them, and re-layouts  2.19 us
  transfers between devices with their start and end apart: 16, of which 10 were waited for; matrix products, arithmetic and copies ran while one was open for 4% of the time, Pallas kernels for 5%

profile of v1, /device:TPU:16, one launch (start us, length us, event | category | flops | bytes accessed | tf_op | source)
XLA Modules:
  0.0 95.8 jit_solution(12291067222113896431)
XLA Ops:
  0.0 1.5 %collective-permute-start.1 = (bf16[256,1024]{1,0:T(8,128)(2,1)}, bf16[256,1024]{1,0:T(8,128)(2,1)S(1)}, u32[]{:S(2)}, u32[]{:S(2)}) collective-permute-start(bf16[256,1024]{1,0:T(8,128)(2,1)} %bitcast.22), channel_id=1, source_target_pairs={{0,16},{8,24},{16,0},{24,8},{1,17},{9,25},{17,1},{25,9},{2,18},{10... | collective-permute-start | bytes 1572872 | tf_op jit(solution)/shard_map/ppermute | solution.py:30
  1.5 1.1 %convolution_convert_fusion = bf16[2,8,128,128]{3,1,2,0:T(8,128)(2,1)S(1)} fusion(bf16[2,8,128,128]{3,2,1,0:T(8,128)(2,1)S(1)} %bitcast.15, s32[2,8]{1,0:T(2,128)} %bitcast.27), kind=kOutput, calls=%fused_computation | convolution fusion | flops 4456576 | bytes 1048640 | tf_op jit(solution)/shard_map/rzk,rzab->rakb/dot_general | solution.py:21
  2.7 1.1 %collective-permute-start.3 = (bf16[256,1024]{1,0:T(8,128)(2,1)S(1)}, bf16[256,1024]{1,0:T(8,128)(2,1)S(1)}, u32[]{:S(2)}, u32[]{:S(2)}) collective-permute-start(bf16[256,1024]{1,0:T(8,128)(2,1)S(1)} %bitcast.19), channel_id=1, source_target_pairs={{0,16},{8,24},{16,0},{24,8},{1,17},{9,25},{17,1},{25,9},{2,18},{10... | collective-permute-start | bytes 1572872 | tf_op jit(solution)/shard_map/ppermute | solution.py:30
  3.8 0.5 collective-permute-start
  5.0 0.7 reduce.1
  5.8 0.9 xor_reduce_fusion
  6.7 0.7 compare_reduce_fusion
  7.5 7.5 %collective-permute-done.1.refs_3_.refs_4_ = bf16[256,1024]{1,0:T(8,128)(2,1)S(1)} collective-permute-done((bf16[256,1024]{1,0:T(8,128)(2,1)}, bf16[256,1024]{1,0:T(8,128)(2,1)S(1)}, u32[]{:S(2)}, u32[]{:S(2)}) %collective-permute-start.1) | collective-permute-done | bytes 524320 | tf_op jit(solution)/shard_map/ppermute | solution.py:30
  15.0 10.1 %collective-permute-done.3.refs_6_ = bf16[256,1024]{1,0:T(8,128)(2,1)S(1)} collective-permute-done((bf16[256,1024]{1,0:T(8,128)(2,1)S(1)}, bf16[256,1024]{1,0:T(8,128)(2,1)S(1)}, u32[]{:S(2)}, u32[]{:S(2)}) %collective-permute-start.3) | collective-permute-done | bytes 524320 | tf_op jit(solution)/shard_map/ppermute | solution.py:30
  25.5 1.0 %copy-done.1 = bf16[1,256,1024]{2,1,0:T(8,128)(2,1)S(1)} copy-done((bf16[1,256,1024]{2,1,0:T(8,128)(2,1)S(1)}, bf16[1,256,1024]{2,1,0:T(8,128)(2,1)}, u32[]{:S(2)}) %copy-start.1) | copy-done | bytes 524312
  26.5 2.5 %early.1 = (bf16[512,1024]{1,0:T(8,128)(2,1)S(1)}, f32[4,8,8,128]{3,2,1,0:T(8,128)S(1)}) custom-call(s32[59]{0:T(128)S(1)} %concatenate.3.refs_0_, bf16[256,1024]{1,0:T(8,128)(2,1)S(1)} %bitcast.24, bf16[256,1024]{1,0:T(8,128)(2,1)S(1)} %collective-permute-done.refs_2_.refs_3_, bf16[256,1024]{1,0:T(8,128)(2,1)S(1)} %collective-permute-done.1.refs_3_.refs_4_, ...), custom_call_target="tpu_custom_call" | custom-call | flops 1073741824 | bytes 4194304 | tf_op jit(solution)/shard_map/early/pallas_call | solution.py:165
  29.0 1.0 %copy-done.2 = bf16[1,256,1024]{2,1,0:T(8,128)(2,1)S(1)} copy-done((bf16[1,256,1024]{2,1,0:T(8,128)(2,1)S(1)}, bf16[1,256,1024]{2,1,0:T(8,128)(2,1)}, u32[]{:S(2)}) %copy-start.2) | copy-done | bytes 524312
  30.1 11.4 %sign.44 = (bf16[768,128]{1,0:T(8,128)(2,1)S(1)}, bf16[768,128]{1,0:T(8,128)(2,1)S(1)}, bf16[768,128]{1,0:T(8,128)(2,1)S(1)}, bf16[768,128]{1,0:T(8,128)(2,1)S(1...) custom-call(s32[59]{0:T(128)S(1)} %concatenate.3.refs_0_, ...), custom_call_target="tpu_custom_call" | custom-call | flops 8153726976 | bytes 31850496 | tf_op jit(solution)/shard_map/sign/pallas_call | solution.py:181
  41.5 1.5 %collective-permute-start.6 = (bf16[768,128]{1,0:T(8,128)(2,1)S(1)}, bf16[768,128]{1,0:T(8,128)(2,1)S(1)}, u32[]{:S(2)}, u32[]{:S(2)}) collective-permute-start(bf16[768,128]{1,0:T(8,128)(2,1)S(1)} %get-tuple-element.22), channel_id=1, source_target_pairs={{0,1},{1,0},{2,3},{3,2},{4,5},{5,4},{6,7},{7,6},{8,9},{9,8},{10,11... | collective-permute-start | bytes 589832 | tf_op jit(solution)/shard_map/ppermute | solution.py:39
  43.0 1.6 %collective-permute-start.7 = (bf16[768,128]{1,0:T(8,128)(2,1)S(1)}, bf16[768,128]{1,0:T(8,128)(2,1)S(1)}, u32[]{:S(2)}, u32[]{:S(2)}) collective-permute-start(bf16[768,128]{1,0:T(8,128)(2,1)S(1)} %get-tuple-element.23), channel_id=1, source_target_pairs={{0,2},{1,3},{2,0},{3,1},{4,6},{5,7},{6,4},{7,5},{8,10},{9,11},{10,... | collective-permute-start | bytes 589832 | tf_op jit(solution)/shard_map/ppermute | solution.py:39
  44.6 0.5 collective-permute-start.8
  45.1 3.7 %collective-permute-start.10 = (bf16[768,128]{1,0:T(8,128)(2,1)S(1)}, bf16[768,128]{1,0:T(8,128)(2,1)S(1)}, u32[]{:S(2)}, u32[]{:S(2)}) collective-permute-start(bf16[768,128]{1,0:T(8,128)(2,1)S(1)} %get-tuple-element.28), channel_id=1, source_target_pairs={{0,5},{1,4},{2,7},{3,6},{4,1},{5,0},{6,3},{7,2},{8,13},{9,12},{10,... | collective-permute-start | bytes 589832 | tf_op jit(solution)/shard_map/ppermute | solution.py:39
  48.9 0.4 collective-permute-start.11
  49.3 6.5 %collective-permute-done.7.refs_4_ = bf16[768,128]{1,0:T(8,128)(2,1)S(1)} collective-permute-done((bf16[768,128]{1,0:T(8,128)(2,1)S(1)}, bf16[768,128]{1,0:T(8,128)(2,1)S(1)}, u32[]{:S(2)}, u32[]{:S(2)}) %collective-permute-start.7) | collective-permute-done | bytes 196640 | tf_op jit(solution)/shard_map/ppermute | solution.py:39
  56.0 3.3 %collective-permute-done.8.refs_5_ = bf16[768,128]{1,0:T(8,128)(2,1)S(1)} collective-permute-done((bf16[768,128]{1,0:T(8,128)(2,1)S(1)}, bf16[768,128]{1,0:T(8,128)(2,1)S(1)}, u32[]{:S(2)}, u32[]{:S(2)}) %collective-permute-start.8) | collective-permute-done | bytes 196640 | tf_op jit(solution)/shard_map/ppermute | solution.py:39
  59.3 1.2 %first.1 = (f32[1,1536]{1,0:T(1,128)S(1)}, bf16[3,768,1536]{2,1,0:T(8,128)(2,1)S(1)}) custom-call(s32[59]{0:T(128)S(1)} %concatenate.3.refs_0_, bf16[6,768,1536]{2,1,0:T(8,128)(2,1)S(1)} %bitcast.18, bf16[768,128]{1,0:T(8,128)(2,1)S(1)} %get-tuple-element.21.refs_2_, bf16[768,128]{1,0:T(8,128)(2,1)S(1)} %collective-permute-done.6.refs_3_, ...), custom_call_target="tpu_custom_call" | custom-call | flops 3019898880 | bytes 11796480 | tf_op jit(solution)/shard_map/first/pallas_call | solution.py:267
  60.5 10.9 %collective-permute-done.10.refs_3_ = bf16[768,128]{1,0:T(8,128)(2,1)S(1)} collective-permute-done((bf16[768,128]{1,0:T(8,128)(2,1)S(1)}, bf16[768,128]{1,0:T(8,128)(2,1)S(1)}, u32[]{:S(2)}, u32[]{:S(2)}) %collective-permute-start.10) | collective-permute-done | bytes 196640 | tf_op jit(solution)/shard_map/ppermute | solution.py:39
  71.4 7.7 %collective-permute-done.11.refs_4_ = bf16[768,128]{1,0:T(8,128)(2,1)S(1)} collective-permute-done((bf16[768,128]{1,0:T(8,128)(2,1)S(1)}, bf16[768,128]{1,0:T(8,128)(2,1)S(1)}, u32[]{:S(2)}, u32[]{:S(2)}) %collective-permute-start.11) | collective-permute-done | bytes 196640 | tf_op jit(solution)/shard_map/ppermute | solution.py:39
  79.1 1.6 %next.1.refs_1_ = f32[1,1536]{1,0:T(1,128)S(1)} custom-call(s32[59]{0:T(128)S(1)} %concatenate.3.refs_0_, f32[1,1536]{1,0:T(1,128)S(1)} %get-tuple-element.26.refs_1_, bf16[3,768,1536]{2,1,0:T(8,128)(2,1)S(1)} %get-tuple-element.27.refs_2_, bf16[768,128]{1,0:T(8,128)(2,1)S(1)} %collective-permute-done.10.refs_3_, ...), custom_call_target="tpu_custom_call" | custom-call | tf_op jit(solution)/shard_map/next/pallas_call | solution.py:286
  80.7 2.3 %collective-permute-done.12.refs_3_ = bf16[768,128]{1,0:T(8,128)(2,1)S(1)} collective-permute-done((bf16[768,128]{1,0:T(8,128)(2,1)S(1)}, bf16[768,128]{1,0:T(8,128)(2,1)S(1)}, u32[]{:S(2)}, u32[]{:S(2)}) %collective-permute-start.12) | collective-permute-done | bytes 196640 | tf_op jit(solution)/shard_map/ppermute | solution.py:39
  83.0 1.1 %last.1 = (f32[4,256]{1,0:T(4,128)S(1)}, f32[4,256]{1,0:T(4,128)S(1)}) custom-call(s32[59]{0:T(128)S(1)} %concatenate.3.refs_0_, f32[1,1536]{1,0:T(1,128)S(1)} %next.1.refs_1_, bf16[3,768,1536]{2,1,0:T(8,128)(2,1)S(1)} %get-tuple-element.27.refs_2_, bf16[768,128]{1,0:T(8,128)(2,1)S(1)} %collective-permute-done.12.refs_3_), custom_call_target="tpu_custom_call" | custom-call | tf_op jit(solution)/shard_map/last/pallas_call | solution.py:298
  84.1 1.6 %collective-permute-start.13 = (f32[4,256]{1,0:T(4,128)S(1)}, f32[4,256]{1,0:T(4,128)S(1)}, u32[]{:S(2)}, u32[]{:S(2)}) collective-permute-start(f32[4,256]{1,0:T(4,128)S(1)} %get-tuple-element.32), channel_id=1, source_target_pairs={{0,16},{8,24},{16,0},{24,8},{1,17},{9,25},{17,1},{25,9},{2,18},{10... | collective-permute-start | bytes 12296 | tf_op jit(solution)/shard_map/ppermute | solution.py:39
  85.6 2.1 %collective-permute-done.13 = f32[4,256]{1,0:T(4,128)S(1)} collective-permute-done((f32[4,256]{1,0:T(4,128)S(1)}, f32[4,256]{1,0:T(4,128)S(1)}, u32[]{:S(2)}, u32[]{:S(2)}) %collective-permute-start.13) | collective-permute-done | bytes 4128 | tf_op jit(solution)/shard_map/ppermute | solution.py:39
  87.7 1.2 %collective-permute-done.14 = f32[2,256]{1,0:T(2,128)S(1)} collective-permute-done((f32[2,256]{1,0:T(2,128)S(1)}, f32[2,256]{1,0:T(2,128)S(1)}, u32[]{:S(2)}, u32[]{:S(2)}) %collective-permute-start.14) | collective-permute-done | bytes 2080 | tf_op jit(solution)/shard_map/ppermute | solution.py:39
  88.9 1.9 %collective-permute-start.15 = (f32[1,256]{1,0:T(1,128)S(1)}, f32[1,256]{1,0:T(1,128)S(1)}, u32[]{:S(2)}, u32[]{:S(2)}) collective-permute-start(f32[1,256]{1,0:T(1,128)S(1)} %slice.19), channel_id=1, source_target_pairs={{0,1},{1,2},{2,3},{3,4},{4,5},{5,6},{6,7},{7,0},{24,31},{25,24},{2... | collective-permute-start | bytes 3080 | tf_op jit(solution)/shard_map/ppermute | solution.py:382
  90.8 4.4 %collective-permute-done.15 = f32[1,256]{1,0:T(1,128)S(1)} collective-permute-done((f32[1,256]{1,0:T(1,128)S(1)}, f32[1,256]{1,0:T(1,128)S(1)}, u32[]{:S(2)}, u32[]{:S(2)}) %collective-permute-start.15) | collective-permute-done | bytes 1056 | tf_op jit(solution)/shard_map/ppermute | solution.py:382
  95.3 0.6 slice_add_fusion.1
  (37 shorter events, 1.0 us)
Async XLA Ops:
  0.0 1.5 %copy-start = (bf16[1,2,8,128,128]{4,3,2,1,0:T(8,128)(2,1)S(1)}, bf16[1,2,8,128,128]{4,3,2,1,0:T(8,128)(2,1)}, u32[]{:S(2)}) copy-start(bf16[1,2,8,128,128]{4,3,2,1,0:T(8,128)(2,1)} %param.8) | copy-start | bytes 1572868
  0.0 15.0 %collective-permute-start.1 = (bf16[256,1024]{1,0:T(8,128)(2,1)}, bf16[256,1024]{1,0:T(8,128)(2,1)S(1)}, u32[]{:S(2)}, u32[]{:S(2)}) collective-permute-start(bf16[256,1024]{1,0:T(8,128)(2,1)} %bitcast.22), channel_id=1, source_target_pairs={{0,16},{8,24},{16,0},{24,8},{1,17},{9,25},{17,1},{25,9},{2,18},{10... | collective-permute-start | bytes 1572872 | tf_op jit(solution)/shard_map/ppermute | solution.py:30
  2.7 22.4 %collective-permute-start.3 = (bf16[256,1024]{1,0:T(8,128)(2,1)S(1)}, bf16[256,1024]{1,0:T(8,128)(2,1)S(1)}, u32[]{:S(2)}, u32[]{:S(2)}) collective-permute-start(bf16[256,1024]{1,0:T(8,128)(2,1)S(1)} %bitcast.19), channel_id=1, source_target_pairs={{0,16},{8,24},{16,0},{24,8},{1,17},{9,25},{17,1},{25,9},{2,18},{10... | collective-permute-start | bytes 1572872 | tf_op jit(solution)/shard_map/ppermute | solution.py:30
  3.8 21.6 %collective-permute-start.5 = (bf16[256,1024]{1,0:T(8,128)(2,1)S(1)}, bf16[256,1024]{1,0:T(8,128)(2,1)S(1)}, u32[]{:S(2)}, u32[]{:S(2)}) collective-permute-start(bf16[256,1024]{1,0:T(8,128)(2,1)S(1)} %bitcast.20), channel_id=1, source_target_pairs={{0,8},{8,0},{16,24},{24,16},{1,9},{9,1},{17,25},{25,17},{2,10},{10... | collective-permute-start | bytes 1572872 | tf_op jit(solution)/shard_map/ppermute | solution.py:39
  3.8 21.6 %collective-permute-start = (bf16[256,1024]{1,0:T(8,128)(2,1)}, bf16[256,1024]{1,0:T(8,128)(2,1)S(1)}, u32[]{:S(2)}, u32[]{:S(2)}) collective-permute-start(bf16[256,1024]{1,0:T(8,128)(2,1)} %bitcast.23), channel_id=1, source_target_pairs={{0,8},{8,0},{16,24},{24,16},{1,9},{9,1},{17,25},{25,17},{2,10},{10... | collective-permute-start | bytes 1572872 | tf_op jit(solution)/shard_map/ppermute | solution.py:39
  15.0 10.4 %collective-permute-start.2 = (bf16[256,1024]{1,0:T(8,128)(2,1)S(1)}, bf16[256,1024]{1,0:T(8,128)(2,1)}, u32[]{:S(2)}, u32[]{:S(2)}) collective-permute-start(bf16[256,1024]{1,0:T(8,128)(2,1)S(1)} %collective-permute-done.1.refs_3_.refs_4_), channel_id=1, source_target_pairs={{0,8},{8,0},{16,24},{24,16},{1,9},{9,1},{17,25},{25,17},{2,10},{10... | collective-permute-start | bytes 1572872 | tf_op jit(solution)/shard_map/ppermute | solution.py:39
  25.1 3.9 %collective-permute-start.4 = (bf16[256,1024]{1,0:T(8,128)(2,1)S(1)}, bf16[256,1024]{1,0:T(8,128)(2,1)}, u32[]{:S(2)}, u32[]{:S(2)}) collective-permute-start(bf16[256,1024]{1,0:T(8,128)(2,1)S(1)} %collective-permute-done.3.refs_6_), channel_id=1, source_target_pairs={{0,8},{8,0},{16,24},{24,16},{1,9},{9,1},{17,25},{25,17},{2,10},{10... | collective-permute-start | bytes 1572872 | tf_op jit(solution)/shard_map/ppermute | solution.py:39
  25.4 1.0 %copy-start.1 = (bf16[1,256,1024]{2,1,0:T(8,128)(2,1)S(1)}, bf16[1,256,1024]{2,1,0:T(8,128)(2,1)}, u32[]{:S(2)}) copy-start(bf16[1,256,1024]{2,1,0:T(8,128)(2,1)} %param.7) | copy-start | bytes 1572868
  26.5 32.8 %slice-start = ((s8[14155776]{0:T(1024)(128)(4,1)}), s8[4194304]{0:T(1024)(128)(4,1)S(1)}, s32[]{:S(2)}) async-start(s8[14155776]{0:T(1024)(128)(4,1)} %bitcast.16), calls=%async_computation | async-start | bytes 8388608
  29.0 1.0 %copy-start.2 = (bf16[1,256,1024]{2,1,0:T(8,128)(2,1)S(1)}, bf16[1,256,1024]{2,1,0:T(8,128)(2,1)}, u32[]{:S(2)}) copy-start(bf16[1,256,1024]{2,1,0:T(8,128)(2,1)} %param.7) | copy-start | bytes 1572868
  30.0 29.2 %slice-start.1 = ((s8[14155776]{0:T(1024)(128)(4,1)}), s8[4194304]{0:T(1024)(128)(4,1)S(1)}, s32[]{:S(2)}) async-start(s8[14155776]{0:T(1024)(128)(4,1)} %bitcast.16), calls=%async_computation.1 | async-start | bytes 8388608
  30.1 29.2 %slice-start.2 = ((s8[14155776]{0:T(1024)(128)(4,1)}), s8[4194304]{0:T(1024)(128)(4,1)S(1)}, s32[]{:S(2)}) async-start(s8[14155776]{0:T(1024)(128)(4,1)} %bitcast.16), calls=%async_computation.2 | async-start | bytes 8388608
  30.1 29.2 %slice-start.3 = ((s8[14155776]{0:T(1024)(128)(4,1)}), s8[1572864]{0:T(1024)(128)(4,1)S(1)}, s32[]{:S(2)}) async-start(s8[14155776]{0:T(1024)(128)(4,1)} %bitcast.16), calls=%async_computation.3 | async-start | bytes 3145728
  41.5 7.4 %collective-permute-start.6 = (bf16[768,128]{1,0:T(8,128)(2,1)S(1)}, bf16[768,128]{1,0:T(8,128)(2,1)S(1)}, u32[]{:S(2)}, u32[]{:S(2)}) collective-permute-start(bf16[768,128]{1,0:T(8,128)(2,1)S(1)} %get-tuple-element.22), channel_id=1, source_target_pairs={{0,1},{1,0},{2,3},{3,2},{4,5},{5,4},{6,7},{7,6},{8,9},{9,8},{10,11... | collective-permute-start | bytes 589832 | tf_op jit(solution)/shard_map/ppermute | solution.py:39
  43.0 12.8 %collective-permute-start.7 = (bf16[768,128]{1,0:T(8,128)(2,1)S(1)}, bf16[768,128]{1,0:T(8,128)(2,1)S(1)}, u32[]{:S(2)}, u32[]{:S(2)}) collective-permute-start(bf16[768,128]{1,0:T(8,128)(2,1)S(1)} %get-tuple-element.23), channel_id=1, source_target_pairs={{0,2},{1,3},{2,0},{3,1},{4,6},{5,7},{6,4},{7,5},{8,10},{9,11},{10,... | collective-permute-start | bytes 589832 | tf_op jit(solution)/shard_map/ppermute | solution.py:39
  44.6 14.7 %collective-permute-start.8 = (bf16[768,128]{1,0:T(8,128)(2,1)S(1)}, bf16[768,128]{1,0:T(8,128)(2,1)S(1)}, u32[]{:S(2)}, u32[]{:S(2)}) collective-permute-start(bf16[768,128]{1,0:T(8,128)(2,1)S(1)} %get-tuple-element.24), channel_id=1, source_target_pairs={{0,3},{1,2},{2,1},{3,0},{4,7},{5,6},{6,5},{7,4},{8,11},{9,10},{10,... | collective-permute-start | bytes 589832 | tf_op jit(solution)/shard_map/ppermute | solution.py:39
  45.0 14.2 %collective-permute-start.9 = (bf16[768,128]{1,0:T(8,128)(2,1)S(1)}, bf16[768,128]{1,0:T(8,128)(2,1)S(1)}, u32[]{:S(2)}, u32[]{:S(2)}) collective-permute-start(bf16[768,128]{1,0:T(8,128)(2,1)S(1)} %get-tuple-element.25), channel_id=1, source_target_pairs={{0,4},{1,5},{2,6},{3,7},{4,0},{5,1},{6,2},{7,3},{8,12},{9,13},{10,... | collective-permute-start | bytes 589832 | tf_op jit(solution)/shard_map/ppermute | solution.py:39
  45.1 26.2 %collective-permute-start.10 = (bf16[768,128]{1,0:T(8,128)(2,1)S(1)}, bf16[768,128]{1,0:T(8,128)(2,1)S(1)}, u32[]{:S(2)}, u32[]{:S(2)}) collective-permute-start(bf16[768,128]{1,0:T(8,128)(2,1)S(1)} %get-tuple-element.28), channel_id=1, source_target_pairs={{0,5},{1,4},{2,7},{3,6},{4,1},{5,0},{6,3},{7,2},{8,13},{9,12},{10,... | collective-permute-start | bytes 589832 | tf_op jit(solution)/shard_map/ppermute | solution.py:39
  48.9 30.2 %collective-permute-start.11 = (bf16[768,128]{1,0:T(8,128)(2,1)S(1)}, bf16[768,128]{1,0:T(8,128)(2,1)S(1)}, u32[]{:S(2)}, u32[]{:S(2)}) collective-permute-start(bf16[768,128]{1,0:T(8,128)(2,1)S(1)} %get-tuple-element.29), channel_id=1, source_target_pairs={{0,6},{1,7},{2,4},{3,5},{4,2},{5,3},{6,0},{7,1},{8,14},{9,15},{10,... | collective-permute-start | bytes 589832 | tf_op jit(solution)/shard_map/ppermute | solution.py:39
  55.8 27.2 %collective-permute-start.12 = (bf16[768,128]{1,0:T(8,128)(2,1)S(1)}, bf16[768,128]{1,0:T(8,128)(2,1)S(1)}, u32[]{:S(2)}, u32[]{:S(2)}) collective-permute-start(bf16[768,128]{1,0:T(8,128)(2,1)S(1)} %get-tuple-element.30), channel_id=1, source_target_pairs={{0,7},{1,6},{2,5},{3,4},{4,3},{5,2},{6,1},{7,0},{8,15},{9,14},{10,... | collective-permute-start | bytes 589832 | tf_op jit(solution)/shard_map/ppermute | solution.py:39
  84.1 3.7 %collective-permute-start.13 = (f32[4,256]{1,0:T(4,128)S(1)}, f32[4,256]{1,0:T(4,128)S(1)}, u32[]{:S(2)}, u32[]{:S(2)}) collective-permute-start(f32[4,256]{1,0:T(4,128)S(1)} %get-tuple-element.32), channel_id=1, source_target_pairs={{0,16},{8,24},{16,0},{24,8},{1,17},{9,25},{17,1},{25,9},{2,18},{10... | collective-permute-start | bytes 12296 | tf_op jit(solution)/shard_map/ppermute | solution.py:39
  87.7 1.2 %collective-permute-start.14 = (f32[2,256]{1,0:T(2,128)S(1)}, f32[2,256]{1,0:T(2,128)S(1)}, u32[]{:S(2)}, u32[]{:S(2)}) collective-permute-start(f32[2,256]{1,0:T(2,128)S(1)} %slice.17), channel_id=1, source_target_pairs={{0,8},{8,0},{16,24},{24,16},{1,9},{9,1},{17,25},{25,17},{2,10},{10... | collective-permute-start | bytes 6152 | tf_op jit(solution)/shard_map/ppermute | solution.py:39
  88.9 6.4 %collective-permute-start.15 = (f32[1,256]{1,0:T(1,128)S(1)}, f32[1,256]{1,0:T(1,128)S(1)}, u32[]{:S(2)}, u32[]{:S(2)}) collective-permute-start(f32[1,256]{1,0:T(1,128)S(1)} %slice.19), channel_id=1, source_target_pairs={{0,1},{1,2},{2,3},{3,4},{4,5},{5,6},{6,7},{7,0},{24,31},{25,24},{2... | collective-permute-start | bytes 3080 | tf_op jit(solution)/shard_map/ppermute | solution.py:382
